TPU v7x, 128 devices: a whole 4x4x4 slice. The times are simulated.
128 devices in a mesh: lat: 4 (over z), lon: 32 (over x, y, core).
Axes of the slice: x: 4, y: 4, z: 4, core: 2. Of those that a mesh axis runs over, the one named last changes fastest.
Arguments:
- fields: bfloat16 [3, 2048, 32, 384], P(None, ('lat', 'lon')), may hold values from -6 to 6
- weights: bfloat16 [3, 4096, 8, 32, 128], P(None, ('lat', 'lon')), may hold values from -0.5 to 0.5
- pair_slots: int32 [3, 4096, 8], P(None, ('lat', 'lon')), may hold values from 0 to 15
- pair_counts: int32 [3, 4096], P(None, ('lat', 'lon')), may hold values from 1 to 8
- requests: int32 [3, 128, 16], replicated, may hold values from 0 to 2047, as said below
- eofs: bfloat16 [200, 524288], P(None, ('lat', 'lon')), may hold values from -0.0078125 to 0.0078125
Outputs:
- pcs: float32 [200, 1152], P(None, ('lat', 'lon'))
Inputs may be any that keep to these rules, and one draw needn't show every extreme that they name: requests[g, d] lists 16 distinct source tiles for grid g and device d (d = lat index * lon devices + lon index); source tile j lies on device j // 16; all of them lie on devices with d's lat index whose lon index is d's own or one of its two cyclic neighbours, at most 8 on any one device, and exactly 8 on some device for every g and d. `pair_slots`: only entries with p < pair_counts[g, t] are used.
All inputs are finite; a program needn't handle non-finite values.
Results may differ from a plain program's by a relative error of at most 0.0029.
Values may be sent and summed in bfloat16 or wider, within the bound.
A program may use at most 128 MiB of HBM per device.

v0:
```python
import jax
import jax.numpy as jnp
from jax import lax
from jax.sharding import PartitionSpec as P

TT = 128
MAXP = 8
MONTHS = 24
MODELS_G = 16
CAP = 8


def from_behind(block, axis, distance):
    devices = range(lax.axis_size(axis))
    route = [((i - distance) % len(devices), i) for i in devices]
    return lax.ppermute(block, axis, route)


def split_up(shard, dim, devices):
    lengths = shard.shape
    parts = shard.reshape(*lengths[:dim], devices, lengths[dim] // devices, *lengths[dim + 1 :])
    return jnp.moveaxis(parts, dim, 0)


def sum_at_owner(shard, axis, dim):
    parts = split_up(shard, dim, lax.axis_size(axis))
    arrived = lax.all_to_all(parts, axis, split_axis=0, concat_axis=0, tiled=True)
    return arrived.sum(axis=0)


def owner_ranks(owners):
    width = owners.shape[-1]
    same = owners[..., :, None] == owners[..., None, :]
    earlier = (
        jnp.arange(width, dtype=jnp.int32)[None, :] < jnp.arange(width, dtype=jnp.int32)[:, None]
    )
    return jnp.sum((same & earlier).astype(jnp.int32), axis=-1)


def sector_offsets(wanted, lat_index, lon_index, lon_count, src_tiles):
    sector = wanted // src_tiles - lat_index * lon_count
    return (sector - lon_index + 1 + lon_count) % lon_count


def shards(fields, weights, pair_slots, pair_counts, requests, eofs):
    lon_count = lax.axis_size("lon")
    lat_index = lax.axis_index("lat")
    lon_index = lax.axis_index("lon")
    device = lat_index * lon_count + lon_index
    grid_count, src_tiles, tile_cells, columns = fields.shape
    tile_total = weights.shape[1]
    wanted = lax.dynamic_index_in_dim(requests, device, 1, keepdims=False)
    grid_rows = jnp.arange(grid_count, dtype=jnp.int32)[:, None]
    local_tiles = wanted % src_tiles
    relative = sector_offsets(wanted, lat_index, lon_index, lon_count, src_tiles)
    slot_range = jnp.arange(CAP, dtype=jnp.int32)

    def selection(neighbour, wanted_rel):
        neighbour_device = lat_index * lon_count + neighbour
        theirs = lax.dynamic_index_in_dim(requests, neighbour_device, 1, keepdims=False)
        their_rel = sector_offsets(theirs, lat_index, neighbour, lon_count, src_tiles)
        their_rank = owner_ranks(their_rel)
        chosen = (their_rel == wanted_rel)[..., None] & (their_rank[..., None] == slot_range)
        picked = jnp.sum(jnp.where(chosen, (theirs % src_tiles)[..., None], 0), axis=1)
        return fields[grid_rows, picked]

    to_right = selection((lon_index + 1) % lon_count, 0)
    to_left = selection((lon_index - 1 + lon_count) % lon_count, 2)
    left_tiles = from_behind(to_right, "lon", 1)
    right_tiles = from_behind(to_left, "lon", -1)
    stacked = jnp.concatenate([left_tiles, fields, right_tiles], axis=1)
    own_rank = owner_ranks(relative)
    position = jnp.where(
        relative == 0,
        own_rank,
        jnp.where(relative == 1, CAP + local_tiles, CAP + src_tiles + own_rank),
    )
    stack_rows = stacked.shape[1]
    row_range = jnp.arange(stack_rows, dtype=jnp.int32)
    pieces = []
    for grid_id in range(grid_count):
        tile_position = position[grid_id][pair_slots[grid_id]]
        live_slots = jnp.arange(MAXP, dtype=jnp.int32)[None, :] < pair_counts[grid_id][:, None]
        selector = ((tile_position[:, :, None] == row_range) & live_slots[:, :, None]).astype(
            jnp.bfloat16
        )
        selector = selector.reshape(tile_total * MAXP, stack_rows)
        source_rows = stacked[grid_id].reshape(stack_rows, tile_cells * columns)
        blocks = jnp.dot(selector, source_rows, preferred_element_type=jnp.float32).astype(
            jnp.bfloat16
        )
        blocks = blocks.reshape(tile_total, MAXP, tile_cells, columns)
        regridded = jnp.einsum(
            "tpsx,tpsc->txc", weights[grid_id], blocks, preferred_element_type=jnp.float32
        )
        by_model = regridded.reshape(tile_total, TT, MODELS_G, MONTHS)
        anomaly = (by_model - jnp.mean(by_model, axis=3, keepdims=True)).astype(jnp.bfloat16)
        anomaly = anomaly.reshape(tile_total * TT, columns)
        pieces.append(jnp.dot(eofs, anomaly, preferred_element_type=jnp.float32))
    partials = jnp.concatenate(pieces, axis=1)
    band_sums = sum_at_owner(partials, "lat", 1)
    return sum_at_owner(band_sums, "lon", 1)


def solution(mesh):
    return jax.shard_map(
        shards,
        mesh=mesh,
        in_specs=(
            P(None, ("lat", "lon"), None, None),
            P(None, ("lat", "lon"), None, None, None),
            P(None, ("lat", "lon"), None),
            P(None, ("lat", "lon")),
            P(),
            P(None, ("lat", "lon")),
        ),
        out_specs=P(None, ("lat", "lon")),
        check_vma=False,
    )
```

profile of v0, /device:TPU:1, one launch (start us, length us, event | category | flops | bytes accessed | tf_op | source)
XLA Modules:
  0.0 190.5 jit_solution(2692236713153587375)
XLA Ops:
  0.0 1.4 dynamic-slice_reduce_fusion.2
  2.0 2.0 %gather_fusion.1 = bf16[24,32,384]{2,1,0:T(8,128)(2,1)S(1)} fusion(bf16[3,16,32,384]{3,2,1,0:T(8,128)(2,1)} %param.6, s32[24]{0:T(128)S(1)} %reshape.462), kind=kCustom, calls=%fused_computation.1 | custom fusion | bytes 1179840 | tf_op jit(solution)/shard_map/gather | solution.py:65
  4.1 2.7 %collective-permute-start = (bf16[3,8,32,384]{3,2,1,0:T(8,128)(2,1)S(1)}, bf16[3,8,32,384]{3,2,1,0:T(8,128)(2,1)S(1)}, u32[]{:S(2)}, u32[]{:S(2)}) collective-permute-start(bf16[3,8,32,384]{3,2,1,0:T(8,128)(2,1)S(1)} %bitcast.155), channel_id=1, source_target_pairs={{31,0},{0,1},{1,2},{2,3},{3,4},{4,5},{5,6},{6,7},{7,8},{8,9},{9,10... | collective-permute-start | bytes 1769480 | tf_op jit(solution)/shard_map/ppermute | solution.py:16
  7.1 2.0 %gather_fusion.2 = bf16[24,32,384]{2,1,0:T(8,128)(2,1)S(1)} fusion(bf16[3,16,32,384]{3,2,1,0:T(8,128)(2,1)} %param.6, s32[24]{0:T(128)S(1)} %reshape.468), kind=kCustom, calls=%fused_computation.2 | custom fusion | bytes 1179840 | tf_op jit(solution)/shard_map/gather | solution.py:65
  9.3 0.7 compare_select_fusion.2
  10.3 0.8 slice_bitcast_fusion.4
  11.7 1.9 gather_fusion.3
  13.6 1.9 gather_fusion
  15.5 2.0 %gather_fusion.4 = s32[256]{0:T(256)S(1)} fusion(s32[16]{0:T(128)S(1)} %get-tuple-element.31, s32[1024]{0:T(1024)S(1)} %get-tuple-element.37), kind=kCustom, calls=%fused_computation.4 | custom fusion | bytes 3072 | tf_op jit(solution)/shard_map/gather | solution.py:82
  17.6 6.7 %fusion.65 = (bf16[1,32,8,32,128]{4,3,2,1,0:T(8,128)(2,1)}, bf16[1,32,8,32,128]{4,3,2,1,0:T(8,128)(2,1)S(1)}, bf16[1,32,8,32,128]{4,3,2,1,0:T(8,128)(2,1)}) fusion(bf16[3,32,8,32,128]{4,3,2,1,0:T(8,128)(2,1)} %param.7), kind=kLoop, calls=%fused_computation.177 | loop fusion | bytes 12582912 | tf_op jit(solution)/shard_map/slice | solution.py:94
  24.6 1.2 constant_dynamic-update-slice_fusion
  26.4 1.8 convolution_convert_fusion.1
  28.2 4.7 %fusion.4 = f32[32,384,128,1]{2,1,3,0:T(8,128)} fusion(bf16[32,8,32,384]{3,1,2,0:T(8,128)(2,1)S(1)} %bitcast.146, bf16[1,32,8,32,128]{4,3,2,1,0:T(8,128)(2,1)S(1)} %get-tuple-element.19), kind=kOutput, calls=%fused_computation.20 | convolution fusion | flops 805306368 | bytes 14680064 | tf_op jit(solution)/shard_map/tpsx,tpsc->txc/dot_general | solution.py:93
  32.9 3.8 %reduce_sum.102 = f32[32,128,16]{1,2,0:T(8,128)S(1)} reduce(f32[32,128,16,24]{1,3,2,0:T(8,128)} %bitcast.133, f32[]{:T(128)} %constant.138.clone.1), dimensions={3}, to_apply=%region_6.7 | reduce | flops 1507328 | bytes 6553604 | tf_op jit(solution)/shard_map/reduce_sum | solution.py:97
  36.9 0.8 sub.177
  37.7 9.0 %copy.81 = f32[48,8,32,128]{3,1,2,0:T(8,128)} copy(f32[48,8,32,128]{3,2,1,0:T(8,128)S(1)} %bitcast.139) | data formatting | bytes 12582912
  46.7 6.6 %copy.49 = f32[4096,384]{1,0:T(8,128)} copy(f32[4096,384]{0,1:T(8,128)} %bitcast.140) | data formatting | bytes 12582912 | tf_op jit(solution)/shard_map/sub | solution.py:97
  53.3 6.5 %copy.47 = f32[32,128,384]{2,1,0:T(8,128)} copy(f32[32,128,384]{1,2,0:T(8,128)} %bitcast.134) | data formatting | bytes 12582912 | tf_op jit(solution)/shard_map/tpsx,tpsc->txc/dot_general | solution.py:93
  60.1 1.8 convolution_convert_fusion.2
  61.9 4.7 %fusion.5 = f32[32,384,128,1]{2,1,3,0:T(8,128)} fusion(bf16[32,8,32,384]{3,1,2,0:T(8,128)(2,1)S(1)} %bitcast.147, bf16[1,32,8,32,128]{4,3,2,1,0:T(8,128)(2,1)S(1)} %copy-done.5), kind=kOutput, calls=%fused_computation.22 | convolution fusion | flops 805306368 | bytes 14680064 | tf_op jit(solution)/shard_map/tpsx,tpsc->txc/dot_general | solution.py:93
  66.6 3.8 %reduce_sum.101 = f32[32,128,16]{1,2,0:T(8,128)S(1)} reduce(f32[32,128,16,24]{1,3,2,0:T(8,128)} %bitcast.135, f32[]{:T(128)} %constant.138.clone.1), dimensions={3}, to_apply=%region_5.6 | reduce | flops 1507328 | bytes 6553604 | tf_op jit(solution)/shard_map/reduce_sum | solution.py:97
  70.5 0.8 sub.174
  71.3 8.7 %copy.82 = f32[48,8,32,128]{3,1,2,0:T(8,128)} copy(f32[48,8,32,128]{3,2,1,0:T(8,128)S(1)} %bitcast.141) | data formatting | bytes 12582912
  80.0 6.7 %copy.44 = f32[4096,384]{1,0:T(8,128)} copy(f32[4096,384]{0,1:T(8,128)} %bitcast.142) | data formatting | bytes 12582912 | tf_op jit(solution)/shard_map/sub | solution.py:97
  86.7 6.6 %copy.42 = f32[32,128,384]{2,1,0:T(8,128)} copy(f32[32,128,384]{1,2,0:T(8,128)} %bitcast.136) | data formatting | bytes 12582912 | tf_op jit(solution)/shard_map/tpsx,tpsc->txc/dot_general | solution.py:93
  93.4 5.6 %fusion.1 = bf16[4096,384]{1,0:T(8,128)(2,1)S(1)} fusion(f32[4096,384]{1,0:T(8,128)} %copy.49, f32[32,128,384]{2,1,0:T(8,128)} %copy.47), kind=kLoop, calls=%fused_computation.14 | loop fusion | flops 3145728 | bytes 15728640 | tf_op jit(solution)/shard_map/convert_element_type | solution.py:97
  99.0 1.0 convolution_bitcast_fusion.1
  100.1 1.5 copy-done.2
  101.6 1.6 fusion.2
  103.2 1.0 convolution_bitcast_fusion.2
  104.5 1.8 convolution_convert_fusion
  106.3 4.8 %fusion.3 = f32[32,384,128,1]{2,1,3,0:T(8,128)} fusion(bf16[32,8,32,384]{3,1,2,0:T(8,128)(2,1)S(1)} %bitcast.145, bf16[1,32,8,32,128]{4,3,2,1,0:T(8,128)(2,1)S(1)} %copy-done.4), kind=kOutput, calls=%fused_computation.18 | convolution fusion | flops 805306368 | bytes 14680064 | tf_op jit(solution)/shard_map/tpsx,tpsc->txc/dot_general | solution.py:93
  111.1 3.8 %reduce_sum.103 = f32[32,128,16]{1,2,0:T(8,128)S(1)} reduce(f32[32,128,16,24]{1,3,2,0:T(8,128)} %bitcast.137, f32[]{:T(128)} %constant.138.clone.1), dimensions={3}, to_apply=%region_7.8 | reduce | flops 1507328 | bytes 6553604 | tf_op jit(solution)/shard_map/reduce_sum | solution.py:97
  115.0 0.8 sub.180
  115.8 8.8 %copy.80 = f32[48,8,32,128]{3,1,2,0:T(8,128)} copy(f32[48,8,32,128]{3,2,1,0:T(8,128)S(1)} %bitcast.143) | data formatting | bytes 12582912
  124.6 6.5 %copy.54 = f32[4096,384]{1,0:T(8,128)} copy(f32[4096,384]{0,1:T(8,128)} %bitcast.144) | data formatting | bytes 12582912 | tf_op jit(solution)/shard_map/sub | solution.py:97
  131.1 6.6 %copy.52 = f32[32,128,384]{2,1,0:T(8,128)} copy(f32[32,128,384]{1,2,0:T(8,128)} %bitcast.138) | data formatting | bytes 12582912 | tf_op jit(solution)/shard_map/tpsx,tpsc->txc/dot_general | solution.py:93
  137.7 5.5 %fusion = bf16[4096,384]{1,0:T(8,128)(2,1)S(1)} fusion(f32[4096,384]{1,0:T(8,128)} %copy.54, f32[32,128,384]{2,1,0:T(8,128)} %copy.52), kind=kLoop, calls=%fused_computation.12 | loop fusion | flops 3145728 | bytes 15728640 | tf_op jit(solution)/shard_map/convert_element_type | solution.py:97
  143.2 1.0 convolution_bitcast_fusion
  144.2 1.0 pad_maximum_fusion
  145.2 2.0 %reshape.452 = f32[200,4,288]{2,1,0:T(4,128)S(1)} reshape(f32[200,1152]{1,0:T(8,128)} %pad_maximum_fusion) | data formatting | bytes 1843200 | tf_op jit(solution)/shard_map/reshape | solution.py:21
  147.2 1.7 copy.55
  148.9 17.2 %all_to_all.10 = f32[4,200,288]{1,2,0:T(8,128)S(1)} all-to-all(f32[4,200,288]{1,2,0:T(8,128)} %copy.55), channel_id=1, replica_groups=mesh['lat'=4,'lon'=32] {'lat'}, dimensions={0} | all-to-all | bytes 1843200 | tf_op jit(solution)/shard_map/all_to_all | solution.py:27
  166.2 0.5 reshape.505
  166.7 20.7 %all_to_all.11 = f32[32,1,1800]{2,1,0:T(1,128)S(1)} all-to-all(f32[32,1,1800]{2,1,0:T(1,128)S(1)} %reshape.505), channel_id=1, replica_groups=mesh['lat'=4,'lon'=32] {'lon'}, dimensions={0} | all-to-all | bytes 460800 | tf_op jit(solution)/shard_map/all_to_all | solution.py:27
  187.4 0.5 broadcast.687
  187.9 1.2 reduce.12
  189.6 0.7 bitcast_reduce_fusion
  (56 shorter events, 4.3 us)
Async XLA Ops:
  0.0 99.0 %copy-start = (bf16[200,4096]{1,0:T(8,128)(2,1)S(1)}, bf16[200,4096]{1,0:T(8,128)(2,1)}, u32[]{:S(2)}) copy-start(bf16[200,4096]{1,0:T(8,128)(2,1)} %param.11) | copy-start | bytes 4915204
  4.1 20.2 %collective-permute-start = (bf16[3,8,32,384]{3,2,1,0:T(8,128)(2,1)S(1)}, bf16[3,8,32,384]{3,2,1,0:T(8,128)(2,1)S(1)}, u32[]{:S(2)}, u32[]{:S(2)}) collective-permute-start(bf16[3,8,32,384]{3,2,1,0:T(8,128)(2,1)S(1)} %bitcast.155), channel_id=1, source_target_pairs={{31,0},{0,1},{1,2},{2,3},{3,4},{4,5},{5,6},{6,7},{7,8},{8,9},{9,10... | collective-permute-start | bytes 1769480 | tf_op jit(solution)/shard_map/ppermute | solution.py:16
  9.1 15.5 %collective-permute-start.1 = (bf16[3,8,32,384]{3,2,1,0:T(8,128)(2,1)S(1)}, bf16[3,8,32,384]{3,2,1,0:T(8,128)(2,1)}, u32[]{:S(2)}, u32[]{:S(2)}) collective-permute-start(bf16[3,8,32,384]{3,2,1,0:T(8,128)(2,1)S(1)} %bitcast.156), channel_id=1, source_target_pairs={{1,0},{2,1},{3,2},{4,3},{5,4},{6,5},{7,6},{8,7},{9,8},{10,9},{11,1... | collective-permute-start | bytes 1769480 | tf_op jit(solution)/shard_map/ppermute | solution.py:16
  17.6 6.8 %copy-start.3 = (bf16[3,16,32,384]{3,2,1,0:T(8,128)(2,1)S(1)}, bf16[3,16,32,384]{3,2,1,0:T(8,128)(2,1)}, u32[]{:S(2)}) copy-start(bf16[3,16,32,384]{3,2,1,0:T(8,128)(2,1)} %param.6) | copy-start | bytes 3538948
  60.1 1.9 copy-start.5
  93.4 6.7 %copy-start.1 = (f32[4096,384]{1,0:T(8,128)S(1)}, f32[4096,384]{1,0:T(8,128)}, u32[]{:S(2)}) copy-start(f32[4096,384]{1,0:T(8,128)} %copy.44) | copy-start | bytes 18874372
  93.4 8.2 %copy-start.2 = (f32[32,128,384]{2,1,0:T(8,128)S(1)}, f32[32,128,384]{2,1,0:T(8,128)}, u32[]{:S(2)}) copy-start(f32[32,128,384]{2,1,0:T(8,128)} %copy.42) | copy-start | bytes 18874372
  104.5 1.9 copy-start.4
where the time goes:
time: 194 us; the launch traced here: 190 us
  local copies, waits for them, and re-layouts  96.3 us (50%)
  blocking collectives  37.9 us (20%)
  other arithmetic  30 us (15%)
  matrix products  22.8 us (12%)
  starting transfers between devices  2.82 us (1%)
    all_to_all x2, blocking collectives, sum_at_owner(): lax.all_to_all(parts, axis, split_axis=0, concat_axis=0, tiled=True)  37.9 us
    unnamed x23, local copies, waits for them, and re-layouts  30 us
    sub x6, local copies, waits for them, and re-layouts, shards(): by_model - jnp.mean(by_model, axis=3, keepdims=True)  22.2 us
    dot_general x3, local copies, waits for them, and re-layouts, shards(): jnp.einsum('tpsx,tpsc->txc', weights[grid_id], blocks, preferred_element_...  19.8 us
    dot_general x3, matrix products, shards(): jnp.einsum('tpsx,tpsc->txc', weights[grid_id], blocks, preferred_element_...  14.2 us
    convert_element_type x3, other arithmetic, shards(): (by_model - jnp.mean(by_model, axis=3, keepdims=True)).astype(jnp.bfloat16)  12.7 us
    reduce_sum x3, other arithmetic, shards(): jnp.mean(by_model, axis=3, keepdims=True)  11.3 us
    slice x1, local copies, waits for them, and re-layouts, shards(): weights[grid_id]  6.7 us
  transfers between devices with their start and end apart: 2, of which 0 were waited for; matrix products, arithmetic and copies ran while one was open for 9% of the time, Pallas kernels for 0%

commit v1 on v0

v1 whole, which is shorter than its diff:
```python
import functools

import jax
import jax.numpy as jnp
from jax import lax
from jax.experimental import pallas as pl
from jax.experimental.pallas import tpu as pltpu
from jax.sharding import PartitionSpec as P

MESH = pl.DeviceIdType.MESH
GRIDS, TILES, PAIRS, TS, TT = 3, 32, 8, 32, 128
STILES, CAP, COLS, EOFS = 16, 8, 384, 200
N_LAT, N_LON = 4, 32
DEVS = N_LAT * N_LON
OWN = 9
MONTHS = 24
GROUPS = 8
F32 = jnp.float32
BF16 = jnp.bfloat16


def pick(value, table):
    out = jnp.int32(table[-1])
    for index, entry in enumerate(table[:-1]):
        out = jnp.where(value == index, jnp.int32(entry), out)
    return out


def body(
    sel, code, fields, weights, eofs, out,
    fld, send, halo, wv, ev, gv, lhs, av, ft, pv, tails, outbox, inbox,
    sem_f, sem_w, sem_e, halo_s, halo_r, x_sem, z_sem, rs_s, rs_r,
):
    lat = lax.axis_index("lat")
    lon = lax.axis_index("lon")
    me = lat * N_LON + lon
    x = lon // 8
    inner = lon % 8
    right = lax.rem(lon + 1, N_LON)
    left = lax.rem(lon + N_LON - 1, N_LON)

    def lon_peer(step):
        return lax.rem(x + step, 4) * 8 + inner

    def group_peer(step):
        return x * 8 + lax.rem(inner + step, 8)

    barrier = pltpu.get_barrier_semaphore()

    def greet(to_lat, to_lon):
        pl.semaphore_signal(barrier, inc=1, device_id=(to_lat, to_lon), device_id_type=MESH)

    for step in range(1, 8):
        greet(lat, group_peer(step))
    greet(lat, left)
    greet(lat, right)
    for step in range(1, 4):
        greet(lat, lon_peer(step))
        greet(lax.rem(lat + step, 4), lon)

    field_copy = pltpu.make_async_copy(fields, fld, sem_f)
    field_copy.start()

    def e_copy(c):
        return pltpu.make_async_copy(
            eofs.at[:, pl.ds(pl.multiple_of(c * 512, 512), 512)], ev.at[c], sem_e.at[c]
        )

    def w_copy(c):
        return pltpu.make_async_copy(
            weights.at[:, pl.ds(c * 4, 4)], wv.at[c], sem_w.at[c]
        )

    @pl.loop(0, GROUPS)
    def _(c):
        e_copy(c).start()
        w_copy(c).start()

    rows = lax.broadcasted_iota(jnp.int32, (192, 256), 0)

    @pl.loop(0, GRIDS * GROUPS)
    def _(i):
        hit = rows == code[i]
        lhs[i] = jnp.where(hit, 1.0, 0.0).astype(BF16)

    field_copy.wait()
    for g in range(GRIDS):
        for way in range(2):
            for r in range(CAP):
                tile = sel[(2 * way * GRIDS + g) * CAP + r]
                send[way, g, pl.ds(r * TS, TS), :] = fld[g * STILES + tile]
    pl.semaphore_wait(barrier, 15)

    def halo_copy(way, g):
        return pltpu.make_async_remote_copy(
            src_ref=send.at[way, g],
            dst_ref=halo.at[way, g],
            send_sem=halo_s.at[way, g],
            recv_sem=halo_r.at[way, g],
            device_id=(lat, right if way == 0 else left),
            device_id_type=MESH,
        )

    for g in range(GRIDS):
        halo_copy(0, g).start()
        halo_copy(1, g).start()
    for step in range(1, 4):
        pl.semaphore_signal(x_sem, inc=1, device_id=(lat, lon_peer(step)), device_id_type=MESH)

    @pl.loop(0, GROUPS)
    def _(c):
        e_copy(c).wait()
        w_copy(c).wait()
        for tt in range(4):
            basis = ev[c, :, tt * TT : (tt + 1) * TT]
            for g in range(GRIDS):
                made = lax.dot_general(
                    wv[c, g, tt], basis, (((1,), (1,)), ((), ())), preferred_element_type=F32
                )
                wide = jnp.concatenate([made, jnp.zeros((256, 56), F32)], axis=1)
                gv[g, c, pl.ds(tt * 8, 8)] = wide.reshape(8, 4, 8, 256)

    pl.semaphore_wait(x_sem, 3)
    for step in range(1, 4):
        pl.semaphore_signal(
            z_sem, inc=1, device_id=(lax.rem(lat + step, 4), lon), device_id_type=MESH
        )

    for g in range(GRIDS):
        @pl.loop(0, 4)
        def _(q):
            total = jnp.zeros((192, 256), F32)
            for c in range(GROUPS):
                terms = gv[g, c, :, q].reshape(256, 256)
                high = terms.astype(BF16)
                low = (terms - high.astype(F32)).astype(BF16)
                chosen = lhs[g * GROUPS + c]
                total += jnp.dot(chosen, high, preferred_element_type=F32)
                total += jnp.dot(chosen, low, preferred_element_type=F32)
            av[g, :, q] = total.reshape(24, 8, 256)

    for g in range(GRIDS):
        own = jnp.concatenate(
            [fld[g * STILES + sel[(GRIDS + g) * CAP + r]] for r in range(CAP)], axis=0
        )
        ft[g] = own.T

    pl.semaphore_wait(z_sem, 3)

    for g in range(GRIDS):
        halo_copy(0, g).wait_recv()
        halo_copy(1, g).wait_recv()
        product = jnp.zeros((COLS, 256), F32)
        for part in range(3):
            source = av[g, pl.ds(part * CAP, CAP)].reshape(256, 256)
            high = source.astype(BF16)
            low = (source - high.astype(F32)).astype(BF16)
            turned = ft[g] if part == 1 else halo[part // 2, g].T
            product += jnp.dot(turned, high, preferred_element_type=F32)
            product += jnp.dot(turned, low, preferred_element_type=F32)
        by_model = product.reshape(COLS // MONTHS, MONTHS, 256)
        centred = by_model - jnp.sum(by_model, axis=1, keepdims=True) * (1.0 / MONTHS)
        centred = centred.reshape(COLS, 256)
        pv[0, pl.ds(g * COLS, COLS), :] = centred[:, :128]
        pv[1, pl.ds(g * COLS, COLS), :] = centred[:, 128:]

    lanes = lax.broadcasted_iota(jnp.int32, (8, 128), 1)

    @pl.loop(0, 16)
    def _(i):
        base = pl.multiple_of(i * 72, 8)
        last = [pv[half, pl.ds(base + 8, 8, stride=9), :] for half in range(2)]
        for r, (half, shift) in enumerate(((0, 72), (0, 16), (0, 88), (1, 72), (1, 16))):
            tails[i, pl.ds(r, 8, stride=8), :] = pltpu.roll(last[half], shift, 1)
        for r in range(5, 8):
            tails[i, pl.ds(r, 8, stride=8), :] = jnp.zeros((8, 128), F32)
        for j in range(8):
            first = pv[0, pl.ds(base + 9 * j, 8), :]
            second = jnp.where(
                lanes < 72, pv[1, pl.ds(base + 9 * j, 8), :], tails[i, 8 * j : 8 * j + 8, :]
            )
            outbox[i * 8 + j] = jnp.concatenate([first, second], axis=0).astype(BF16)

    def owner_copy(to_lat, to_lon):
        return pltpu.make_async_remote_copy(
            src_ref=outbox.at[to_lat * N_LON + to_lon],
            dst_ref=inbox.at[me],
            send_sem=rs_s,
            recv_sem=rs_r,
            device_id=(to_lat, to_lon),
            device_id_type=MESH,
        )

    order = (2, 1, 3, 0)

    @pl.loop(0, DEVS - 1)
    def _(i):
        to_lat = lax.rem(lat + pick(i // 32, order), 4)
        to_x = lax.rem(x + pick(lax.rem(i // 8, 4), order), 4)
        to_y = lax.rem(inner // 2 + pick(lax.rem(i // 2, 4), order), 4)
        to_core = lax.rem(inner + 1 + i, 2)
        owner_copy(to_lat, to_x * 8 + to_y * 2 + to_core).start()

    inbox[me] = outbox[me]
    everything = pltpu.make_async_remote_copy(
        src_ref=outbox.at[pl.ds(0, DEVS - 1)],
        dst_ref=inbox.at[pl.ds(0, DEVS - 1)],
        send_sem=rs_s,
        recv_sem=rs_r,
        device_id=(lat, right),
        device_id_type=MESH,
    )
    everything.wait_recv()
    total = jnp.zeros((16, 128), F32)
    for i in range(DEVS):
        total += inbox[i].astype(F32)
    out[...] = total

    everything.wait_send()
    for g in range(GRIDS):
        halo_copy(0, g).wait_send()
        halo_copy(1, g).wait_send()


def tables(pair_slots, pair_counts, requests):
    lat = lax.axis_index("lat")
    lon = lax.axis_index("lon")
    me = lat * N_LON + lon
    left = lat * N_LON + (lon + N_LON - 1) % N_LON
    right = lat * N_LON + (lon + 1) % N_LON
    row = lambda d: lax.dynamic_index_in_dim(requests, d, 1, keepdims=False)
    wanted = jnp.stack([row(right), row(me), row(left)])
    count = wanted.shape[-1]
    slots = jnp.arange(count, dtype=jnp.int32)
    earlier = slots[None, :] < slots[:, None]
    owner = wanted // STILES
    rank = jnp.sum(((owner[..., :, None] == owner[..., None, :]) & earlier).astype(jnp.int32), axis=-1)
    mine = (owner == me)[..., None] & (rank[..., None] == jnp.arange(CAP, dtype=jnp.int32))
    sel = jnp.sum(jnp.where(mine, (wanted % STILES)[..., None], 0), axis=2)
    own = owner[1]
    place = jnp.where(own == left, 0, jnp.where(own == me, CAP, 2 * CAP)) + rank[1]
    flat = pair_slots.reshape(GRIDS, TILES * PAIRS)
    position = jnp.sum(jnp.where(flat[..., None] == slots, place[:, None, :], 0), axis=-1)
    live = (jnp.arange(PAIRS, dtype=jnp.int32) < pair_counts[..., None]).reshape(GRIDS, TILES * PAIRS)
    eight = jnp.arange(8, dtype=jnp.int32)
    code = jnp.where(live, position * 8, -8)[..., None] + eight
    return sel.reshape(-1), code.reshape(GRIDS * GROUPS, 1, 256)


def shards(fields, weights, pair_slots, pair_counts, requests, eofs):
    sel, code = tables(pair_slots, pair_counts, requests)
    anywhere = pl.BlockSpec(memory_space=pl.ANY)
    summed = pl.pallas_call(
        body,
        out_shape=jax.ShapeDtypeStruct((16, 128), F32),
        in_specs=[
            pl.BlockSpec(memory_space=pltpu.SMEM),
            pl.BlockSpec(memory_space=pltpu.VMEM),
            anywhere,
            anywhere,
            anywhere,
        ],
        out_specs=pl.BlockSpec(memory_space=pltpu.VMEM),
        scratch_shapes=[
            pltpu.VMEM((GRIDS * STILES, TS, COLS), BF16),
            pltpu.VMEM((2, GRIDS, CAP * TS, COLS), BF16),
            pltpu.VMEM((2, GRIDS, CAP * TS, COLS), BF16),
            pltpu.VMEM((GROUPS, GRIDS, 4, 256, TT), BF16),
            pltpu.VMEM((GROUPS, EOFS, 512), BF16),
            pltpu.VMEM((GRIDS, GROUPS, 32, 4, 8, 256), F32),
            pltpu.VMEM((GRIDS * GROUPS, 192, 256), BF16),
            pltpu.VMEM((GRIDS, 24, 4, 8, 256), F32),
            pltpu.VMEM((GRIDS, COLS, 256), BF16),
            pltpu.VMEM((2, GRIDS * COLS + 8, 128), F32),
            pltpu.VMEM((16, 64, 128), F32),
            pltpu.VMEM((DEVS, 16, 128), BF16),
            pltpu.VMEM((DEVS, 16, 128), BF16),
            pltpu.SemaphoreType.DMA,
            pltpu.SemaphoreType.DMA((GROUPS,)),
            pltpu.SemaphoreType.DMA((GROUPS,)),
            pltpu.SemaphoreType.DMA((2, GRIDS)),
            pltpu.SemaphoreType.DMA((2, GRIDS)),
            pltpu.SemaphoreType.REGULAR,
            pltpu.SemaphoreType.REGULAR,
            pltpu.SemaphoreType.DMA,
            pltpu.SemaphoreType.DMA,
        ],
        compiler_params=pltpu.CompilerParams(
            collective_id=0, has_side_effects=True, vmem_limit_bytes=56 * 1024 * 1024
        ),
    )(
        sel,
        code,
        fields.reshape(GRIDS * STILES, TS, COLS),
        weights.reshape(GRIDS, TILES, PAIRS * TS, TT),
        eofs,
    )
    last = jnp.concatenate(
        [summed[8, 72:], summed[9, 72:], summed[10, 72:88], summed[11, 72:], summed[12, 72:88]]
    )
    first = jnp.concatenate([summed[:8], summed[8:, :72]], axis=1)
    return jnp.concatenate([first, last[None]], axis=0).T


def solution(mesh):
    return jax.shard_map(
        shards,
        mesh=mesh,
        in_specs=(
            P(None, ("lat", "lon"), None, None),
            P(None, ("lat", "lon"), None, None, None),
            P(None, ("lat", "lon"), None),
            P(None, ("lat", "lon")),
            P(),
            P(None, ("lat", "lon")),
        ),
        out_specs=P(None, ("lat", "lon")),
        check_vma=False,
    )
```

time: 194 us -> 44.3 us (0.23); the launches traced: 190 us -> 43.8 us
  local copies, waits for them, and re-layouts: 96.3 us -> 7.56 us
  blocking collectives: 37.9 us -> 0 us
  Pallas kernels: 0 us -> 34.7 us
  other arithmetic: 30 us -> 1.5 us
  matrix products: 22.8 us -> 0 us
  starting transfers between devices: 2.82 us -> 0 us
    all_to_all x2 -> x0, blocking collectives: 37.9 us -> none  [sum_at_owner(): lax.all_to_all(parts, axis, split_axis=0, concat_axis=0, tiled=True)]
    pallas_call x0 -> x1, Pallas kernels: none -> 34.7 us  [shards(): pl.pallas_call(body, out_shape=jax.ShapeDtypeStruct((16, 128), F32), in_s...]
    unnamed x23 -> x1, local copies, waits for them, and re-layouts: 30 us -> 0.79 us
    dot_general x9 -> x0, matrix products: 22.8 us -> none  [the longest x3 14.2 us: shards(): jnp.einsum('tpsx,tpsc->txc', weights[grid_id], blocks, preferred_element_...]
    sub x6 -> x0, local copies, waits for them, and re-layouts: 22.2 us -> none  [shards(): by_model - jnp.mean(by_model, axis=3, keepdims=True)]
    dot_general x3 -> x0, local copies, waits for them, and re-layouts: 19.8 us -> none  [shards(): jnp.einsum('tpsx,tpsc->txc', weights[grid_id], blocks, preferred_element_...]
    convert_element_type x3 -> x0, other arithmetic: 12.7 us -> none  [shards(): (by_model - jnp.mean(by_model, axis=3, keepdims=True)).astype(jnp.bfloat16)]
    reduce_sum x8 -> x3, other arithmetic: 12.7 us -> 0.67 us  [the longest x1 0.33 us: tables(): jnp.sum(((owner[..., :, None] == owner[..., None, :]) & earlier).astype(j...]
  transfers between devices with their start and end apart: 2 -> 0, of which waited for: 0 -> 0; matrix products, arithmetic and copies ran while one was open for 9% -> 0% of each run, Pallas kernels for 0% -> 0%
where the time goes in v1:
time: 44.3 us; the launch traced here: 43.8 us
  Pallas kernels  34.7 us (78%)
  local copies, waits for them, and re-layouts  7.56 us (17%)
  other arithmetic  1.5 us (3%)
    pallas_call x1, Pallas kernels, shards(): pl.pallas_call(body, out_shape=jax.ShapeDtypeStruct((16, 128), F32), in_s...  34.7 us
    slice x2, local copies, waits for them, and re-layouts, shards(): first = jnp.concatenate([summed[:8], summed[8:, :72]], axis=1)  1.35 us
    dynamic_slice x1, local copies, waits for them, and re-layouts, tables(): row = lambda d: lax.dynamic_index_in_dim(requests, d, 1, keepdims=False)  1.18 us
    lt x4, local copies, waits for them, and re-layouts, tables(): jnp.arange(PAIRS, dtype=jnp.int32) < pair_counts[..., None]  0.95 us

profile of v1, /device:TPU:1, one launch (start us, length us, event | category | flops | bytes accessed | tf_op | source)
XLA Modules:
  0.0 43.8 jit_solution(15604909352936440494)
XLA Ops:
  0.0 1.2 %dynamic-slice_reduce_fusion.2 = (s32[3,16]{1,0:T(4,128)S(1)}, s32[3,16]{1,0:T(4,128)S(1)}, s32[3,16]{1,0:T(4,128)S(1)}) fusion(s32[3,128,16]{1,2,0:T(8,128)} %param.10, s32[]{:T(128)S(6)} %select_n.82, s32[]{:T(128)S(6)} %select_n.85, s32[]{:T(128)S(6)} %select_n.83), kind=kLoop, calls=%fused_computation.9 | loop fusion | bytes 1164 | tf_op jit(solution)/shard_map/jit(dynamic_index_in_dim)/dynamic_slice | solution.py:231
  1.2 0.3 convert_reduce_fusion
  1.6 0.3 select_reduce_fusion.1
  1.8 0.6 %reshape.409.sel = s32[72]{0:T(128)} reshape(s32[3,3,8]{2,1,0:T(4,128)S(1)} %select_reduce_fusion.1) | data formatting | bytes 576 | tf_op jit(solution)/shard_map/reshape | solution.py:247
  2.4 0.1 lt.77
  2.5 0.8 %copy.22 = s32[3,32,8]{2,1,0:T(8,128)S(1)} copy(s32[3,32,8]{1,2,0:T(8,128)} %param.8) | data formatting | bytes 6144 | tf_op args[2]
  3.3 0.1 eq.86
  3.4 0.1 select_reduce_fusion
  3.5 0.8 %lt.79 = s32[3,32,8]{2,1,0:T(8,128)S(1)} broadcast(s32[3,32]{1,0:T(4,128)} %param.9), dimensions={0,1} | broadcast | bytes 3456 | tf_op jit(solution)/shard_map/lt | solution.py:244
  4.3 0.1 lt.80
  4.4 0.2 iota_add_fusion
  4.6 0.8 %add.104.code = s32[24,1,256]{2,1,0:T(1,128)} reshape(s32[3,256,8]{2,1,0:T(8,128)S(1)} %iota_add_fusion) | data formatting | bytes 49152 | tf_op jit(solution)/shard_map/add | solution.py:246
  5.4 34.7 %shard_map.64 = f32[16,128]{1,0:T(8,128)} custom-call(s32[72]{0:T(128)} %reshape.409.sel, s32[24,1,256]{2,1,0:T(1,128)} %add.104.code, bf16[48,32,384]{2,1,0:T(8,128)(2,1)} %bitcast.21, bf16[3,32,256,128]{3,2,1,0:T(8,128)(2,1)} %bitcast.20, bf16[200,4096]{1,0:T(8,128)(2,1)} %eofs.1), custom_call_target="tpu_custom_call" | custom-call | tf_op jit(solution)/shard_map/pallas_call | solution.py:253
  40.1 0.8 %slice_bitcast_fusion = (f32[16]{0:T(128)S(1)}, f32[16]{0:T(128)S(1)}) fusion(f32[16,128]{1,0:T(8,128)} %shard_map.64), kind=kLoop, calls=%fused_computation.25 | loop fusion | bytes 256 | tf_op jit(solution)/shard_map/squeeze | solution.py:299
  40.9 0.9 %slice_bitcast_fusion.1 = (f32[56]{0:T(128)S(1)}, f32[56]{0:T(128)S(1)}, f32[56]{0:T(128)S(1)}) fusion(f32[16,128]{1,0:T(8,128)} %shard_map.64), kind=kLoop, calls=%fused_computation.26 | loop fusion | bytes 1344 | tf_op jit(solution)/shard_map/squeeze | solution.py:299
  41.8 0.1 concatenate.55
  41.9 0.7 %slice.30 = f32[8,72]{1,0:T(8,128)S(1)} slice(f32[16,128]{1,0:T(8,128)} %shard_map.64), slice={[8:16], [0:72]} | slice | bytes 4608 | tf_op jit(solution)/shard_map/slice | solution.py:301
  42.6 0.7 %slice.29 = f32[8,128]{1,0:T(8,128)S(1)} slice(f32[16,128]{1,0:T(8,128)} %shard_map.64), slice={[0:8], [0:128]} | slice | bytes 8192 | tf_op jit(solution)/shard_map/slice | solution.py:301
  43.2 0.6 %maximum_bitcast_fusion = f32[200,9]{0,1:T(8,128)} fusion(f32[1,200]{1,0:T(1,128)S(1)} %bitcast.28, f32[8,72]{1,0:T(8,128)S(1)} %slice.30, f32[8,128]{1,0:T(8,128)S(1)} %slice.29), kind=kLoop, calls=%fused_computation.10 | loop fusion | flops 3600 | bytes 14400 | tf_op jit(solution)/shard_map/transpose | solution.py:302
  (6 shorter events, 0.1 us)

commit v2 on v0

v2 whole, which is shorter than its diff:
```python
import jax
import jax.numpy as jnp
from jax import lax
from jax.experimental import pallas as pl
from jax.experimental.pallas import tpu as pltpu
from jax.sharding import PartitionSpec as P

MESH = pl.DeviceIdType.MESH
GRIDS, TILES, PAIRS, TS, TT = 3, 32, 8, 32, 128
STILES, REQ, CAP, COLS, EOFS = 16, 16, 8, 384, 200
N_LAT, N_LON = 4, 32
DEVS = N_LAT * N_LON
OWN = 9
MONTHS = 24
GROUPS = 8
F32 = jnp.float32
BF16 = jnp.bfloat16
PHASES = ((0, 5), (5, 10), (10, 16))


def body(
    requests, slots, counts, fields, weights, eofs, out,
    wanted, slot_v, count_v, fld, send, halo_0, halo_1, halo_2, wv, ev, gv, lhs, av, pv, tails,
    outbox, inbox,
    sem_i, sem_f, sem_w, sem_e, halo_s, halo_r, x_sem, z_sem, rs_s, rs_r,
):
    lat = lax.axis_index("lat")
    lon = lax.axis_index("lon")
    me = lat * N_LON + lon
    right = (lon + 1) & 31
    left = (lon + 31) & 31
    halos = (halo_0, halo_1, halo_2)

    barrier = pltpu.get_barrier_semaphore()

    def greet(sem, to_lat, to_lon):
        pl.semaphore_signal(sem, inc=1, device_id=(to_lat, to_lon), device_id_type=MESH)

    with jax.named_scope("greet"):
        greet(barrier, lat, left)
        greet(barrier, lat, right)
        for step in range(1, 8):
            greet(barrier, lat, lon ^ step)
        for step in range(1, 4):
            greet(barrier, lat, lon ^ (step * 8))
            greet(barrier, lat ^ step, lon)

        inputs = [
            pltpu.make_async_copy(requests, wanted, sem_i.at[0]),
            pltpu.make_async_copy(slots, slot_v, sem_i.at[1]),
            pltpu.make_async_copy(counts, count_v, sem_i.at[2]),
        ]
        for copy in inputs:
            copy.start()
        field_copy = pltpu.make_async_copy(fields, fld, sem_f)
        field_copy.start()

    def e_copy(c):
        return pltpu.make_async_copy(
            eofs.at[:, pl.ds(pl.multiple_of(c * 512, 512), 512)], ev.at[c], sem_e.at[c]
        )

    def w_copy(c):
        return pltpu.make_async_copy(weights.at[:, pl.ds(c * 4, 4)], wv.at[c], sem_w.at[c])

    @pl.loop(0, GROUPS)
    def _(c):
        e_copy(c).start()
        w_copy(c).start()

    with jax.named_scope("codes"):
        inputs[1].wait()
        inputs[2].wait()
        live = lax.broadcasted_iota(jnp.int32, (GRIDS, PAIRS, TILES), 1) < count_v[...][:, None, :]
        marked = jnp.where(live, slot_v[...] + 1, 0).astype(F32)
        marked = marked.reshape(GRIDS * PAIRS, TILES).astype(BF16)
        lane = lax.broadcasted_iota(jnp.int32, (TILES, TILES * 64), 1)
        tile = lax.broadcasted_iota(jnp.int32, (TILES, TILES * 64), 0)
        spread = jnp.where((lane >> 6) == tile, 1.0, 0.0).astype(BF16)
        codes = jnp.dot(marked, spread, preferred_element_type=F32)
        codes = codes.reshape(GRIDS, PAIRS, TILES * 64)
        lane = lax.broadcasted_iota(jnp.int32, (PAIRS, TILES * 64), 1)
        pair = lax.broadcasted_iota(jnp.int32, (PAIRS, TILES * 64), 0)
        codes = jnp.sum(jnp.where(((lane >> 3) & 7) == pair, codes, 0.0), axis=1)
        row = (lax.broadcasted_iota(jnp.int32, (GRIDS, TILES * 64), 1) & 7).astype(F32)
        codes = codes * 8.0 + (row - 8.0)
        rows = lax.broadcasted_iota(jnp.int32, (128, 256), 0).astype(F32)
        for g in range(GRIDS):
            for c in range(GROUPS):
                hit = rows == codes[g : g + 1, c * 256 : (c + 1) * 256]
                lhs[g * GROUPS + c] = jnp.where(hit, 1.0, 0.0).astype(BF16)

    with jax.named_scope("pick"):
        inputs[0].wait()

        def mine_of(g, device):
            chosen = [jnp.int32(0)] * CAP
            seen = jnp.int32(0)
            for j in range(REQ):
                source = wanted[g * REQ + j, device]
                mine = (source >> 4) == me
                for r in range(min(j + 1, CAP)):
                    chosen[r] = jnp.where(mine & (seen == r), source & 15, chosen[r])
                seen = seen + jnp.where(mine, 1, 0)
            return chosen

        picked = [[mine_of(g, lat * N_LON + to) for g in range(GRIDS)] for to in (right, left)]

    with jax.named_scope("gather"):
        field_copy.wait()
        for g in range(GRIDS):
            for way in range(2):
                for r in range(CAP):
                    send[way, g, r] = fld[g * STILES + picked[way][g][r]]

    def halo_copy(way, g):
        return pltpu.make_async_remote_copy(
            src_ref=send.at[way, g],
            dst_ref=halos[g].at[way],
            send_sem=halo_s.at[way, g],
            recv_sem=halo_r.at[way, g],
            device_id=(lat, right if way == 0 else left),
            device_id_type=MESH,
        )

    def project(c):
        e_copy(c).wait()
        w_copy(c).wait()
        for tt in range(4):
            basis = ev[c, :, tt * TT : (tt + 1) * TT]
            for g in range(GRIDS):
                made = lax.dot_general(
                    wv[c, g, tt], basis, (((1,), (1,)), ((), ())), preferred_element_type=F32
                )
                wide = jnp.concatenate([made, jnp.zeros((256, 56), F32)], axis=1)
                gv[g, c, pl.ds(tt * 8, 8)] = wide.reshape(8, 4, 8, 256)

    with jax.named_scope("barrier"):
        pl.semaphore_wait(barrier, 15)
        for g in range(GRIDS):
            halo_copy(0, g).start()
            halo_copy(1, g).start()
        for step in range(1, 4):
            greet(x_sem, lat, lon ^ (step * 8))

    with jax.named_scope("project"):

        @pl.loop(0, GROUPS)
        def _(c):
            project(c)

    with jax.named_scope("barrier2"):
        pl.semaphore_wait(x_sem, 3)
        for step in range(1, 4):
            greet(z_sem, lat ^ step, lon)

    with jax.named_scope("addup"):
        for g in range(GRIDS):

            @pl.loop(0, 4)
            def _(q):
                total = jnp.zeros((128, 256), F32)
                for c in range(GROUPS):
                    terms = gv[g, c, :, q].reshape(256, 256)
                    high = terms.astype(BF16)
                    low = (terms - high.astype(F32)).astype(BF16)
                    chosen = lhs[g * GROUPS + c]
                    total += jnp.dot(chosen, high, preferred_element_type=F32)
                    total += jnp.dot(chosen, low, preferred_element_type=F32)
                av[g, :, q] = total.reshape(REQ, 8, 256)

    with jax.named_scope("barrier3"):
        pl.semaphore_wait(z_sem, 3)

    lanes = lax.broadcasted_iota(jnp.int32, (8, 128), 1)

    def owner_copy(owner):
        return pltpu.make_async_remote_copy(
            src_ref=outbox.at[owner],
            dst_ref=inbox.at[me],
            send_sem=rs_s,
            recv_sem=rs_r,
            device_id=(owner >> 5, owner & 31),
            device_id_type=MESH,
        )

    for g in range(GRIDS):
        with jax.named_scope(f"halo{g}"):
            halo_copy(0, g).wait_recv()
            halo_copy(1, g).wait_recv()
        with jax.named_scope(f"product{g}"):
            product = jnp.zeros((COLS, 256), F32)
            seen_left = jnp.int32(0)
            seen_right = jnp.int32(0)
            for half in range(2):
                blocks = []
                for j in range(half * 8, half * 8 + 8):
                    source = wanted[g * REQ + j, me]
                    owner = source >> 4
                    on_left = owner == lat * N_LON + left
                    on_me = owner == me
                    from_left = halos[g][0, seen_left & 7]
                    from_right = halos[g][1, seen_right & 7]
                    from_me = fld[g * STILES + (source & 15)]
                    blocks.append(
                        jnp.where(on_me, from_me, jnp.where(on_left, from_left, from_right))
                    )
                    seen_left = seen_left + jnp.where(on_left, 1, 0)
                    seen_right = seen_right + jnp.where(on_left | on_me, 0, 1)
                turned = jnp.concatenate(blocks, axis=0).T
                source = av[g, pl.ds(half * 8, 8)].reshape(256, 256)
                high = source.astype(BF16)
                low = (source - high.astype(F32)).astype(BF16)
                product += jnp.dot(turned, high, preferred_element_type=F32)
                product += jnp.dot(turned, low, preferred_element_type=F32)
            by_model = product.reshape(COLS // MONTHS, MONTHS, 256)
            centred = by_model - jnp.sum(by_model, axis=1, keepdims=True) * (1.0 / MONTHS)
            centred = centred.reshape(COLS, 256)
            pv[0, pl.ds(g * COLS, COLS), :] = centred[:, :128]
            pv[1, pl.ds(g * COLS, COLS), :] = centred[:, 128:]

        start, stop = PHASES[g]
        with jax.named_scope(f"pack{g}"):

            @pl.loop(start, stop)
            def _(i):
                base = pl.multiple_of(i * 72, 8)
                last = [pv[half, pl.ds(base + 8, 8, stride=9), :] for half in range(2)]
                for r, (half, shift) in enumerate(((0, 72), (0, 16), (0, 88), (1, 72), (1, 16))):
                    tails[i, pl.ds(r, 8, stride=8), :] = pltpu.roll(last[half], shift, 1)
                for r in range(5, 8):
                    tails[i, pl.ds(r, 8, stride=8), :] = jnp.zeros((8, 128), F32)
                for j in range(8):
                    first = pv[0, pl.ds(base + 9 * j, 8), :]
                    second = jnp.where(
                        lanes < 72, pv[1, pl.ds(base + 9 * j, 8), :], tails[i, 8 * j : 8 * j + 8, :]
                    )
                    outbox[i * 8 + j] = jnp.concatenate([first, second], axis=0).astype(BF16)

        with jax.named_scope(f"send{g}"):
            count = stop - start
            turn = lax.rem(me >> 3, count)

            @pl.loop(0, count)
            def _(k):
                group = k + turn
                group = start + group - jnp.where(group >= count, count, 0)

                @pl.when(group != me >> 3)
                def _():
                    owner_copy(group * 8 + (me & 7)).start()

                for j in range(1, 8):
                    owner_copy(group * 8 + ((me & 7) ^ j)).start()

    with jax.named_scope("arrive"):
        inbox[me] = outbox[me]
        everything = pltpu.make_async_remote_copy(
            src_ref=outbox.at[pl.ds(0, DEVS - 1)],
            dst_ref=inbox.at[pl.ds(0, DEVS - 1)],
            send_sem=rs_s,
            recv_sem=rs_r,
            device_id=(lat, right),
            device_id_type=MESH,
        )
        everything.wait_recv()
    with jax.named_scope("final"):
        total = jnp.zeros((16, 128), F32)
        for i in range(DEVS):
            total += inbox[i].astype(F32)
        first, second = total[:8], total[8:]
        by_56, by_112, by_40 = (pltpu.roll(second, shift, 1) for shift in (56, 112, 40))
        lane = lanes[:1]
        last_0 = jnp.where(lane < 56, by_56[0:1], jnp.where(lane < 112, by_112[1:2], by_40[2:3]))
        last_1 = jnp.where(lane < 56, by_56[3:4], by_112[4:5])
        out[0:8, 0:128] = first
        out[0:8, 128:EOFS] = second[:, : EOFS - 128]
        out[8:9, 0:128] = last_0
        out[8:9, 128:EOFS] = last_1[:, : EOFS - 128]

    with jax.named_scope("drain"):
        everything.wait_send()
        for g in range(GRIDS):
            halo_copy(0, g).wait_send()
            halo_copy(1, g).wait_send()


def shards(fields, weights, pair_slots, pair_counts, requests, eofs):
    return pl.pallas_call(
        body,
        out_shape=jax.ShapeDtypeStruct((OWN, EOFS), F32),
        in_specs=[pl.BlockSpec(memory_space=pl.ANY)] * 6,
        out_specs=pl.BlockSpec(memory_space=pltpu.VMEM),
        scratch_shapes=[
            pltpu.SMEM((GRIDS * REQ, DEVS), jnp.int32),
            pltpu.VMEM((GRIDS, PAIRS, TILES), jnp.int32),
            pltpu.VMEM((GRIDS, TILES), jnp.int32),
            pltpu.VMEM((GRIDS * STILES, TS, COLS), BF16),
            pltpu.VMEM((2, GRIDS, CAP, TS, COLS), BF16),
            pltpu.VMEM((2, CAP, TS, COLS), BF16),
            pltpu.VMEM((2, CAP, TS, COLS), BF16),
            pltpu.VMEM((2, CAP, TS, COLS), BF16),
            pltpu.VMEM((GROUPS, GRIDS, 4, 256, TT), BF16),
            pltpu.VMEM((GROUPS, EOFS, 512), BF16),
            pltpu.VMEM((GRIDS, GROUPS, 32, 4, 8, 256), F32),
            pltpu.VMEM((GRIDS * GROUPS, 128, 256), BF16),
            pltpu.VMEM((GRIDS, REQ, 4, 8, 256), F32),
            pltpu.VMEM((2, GRIDS * COLS + 8, 128), F32),
            pltpu.VMEM((16, 64, 128), F32),
            pltpu.VMEM((DEVS, 16, 128), BF16),
            pltpu.VMEM((DEVS, 16, 128), BF16),
            pltpu.SemaphoreType.DMA((3,)),
            pltpu.SemaphoreType.DMA,
            pltpu.SemaphoreType.DMA((GROUPS,)),
            pltpu.SemaphoreType.DMA((GROUPS,)),
            pltpu.SemaphoreType.DMA((2, GRIDS)),
            pltpu.SemaphoreType.DMA((2, GRIDS)),
            pltpu.SemaphoreType.REGULAR,
            pltpu.SemaphoreType.REGULAR,
            pltpu.SemaphoreType.DMA,
            pltpu.SemaphoreType.DMA,
        ],
        compiler_params=pltpu.CompilerParams(
            collective_id=0, has_side_effects=True, vmem_limit_bytes=56 * 1024 * 1024
        ),
    )(
        requests.transpose(0, 2, 1).reshape(GRIDS * REQ, DEVS),
        pair_slots.transpose(0, 2, 1),
        pair_counts,
        fields.reshape(GRIDS * STILES, TS, COLS),
        weights.reshape(GRIDS, TILES, PAIRS * TS, TT),
        eofs,
    ).T


def solution(mesh):
    return jax.shard_map(
        shards,
        mesh=mesh,
        in_specs=(
            P(None, ("lat", "lon"), None, None),
            P(None, ("lat", "lon"), None, None, None),
            P(None, ("lat", "lon"), None),
            P(None, ("lat", "lon")),
            P(),
            P(None, ("lat", "lon")),
        ),
        out_specs=P(None, ("lat", "lon")),
        check_vma=False,
    )
```

time: 194 us -> 31.1 us (0.16); the launches traced: 190 us -> 30.9 us
  local copies, waits for them, and re-layouts: 96.3 us -> 1.32 us
  blocking collectives: 37.9 us -> 0 us
  other arithmetic: 30 us -> 0 us
  Pallas kernels: 0 us -> 29.6 us
  matrix products: 22.8 us -> 0 us
  starting transfers between devices: 2.82 us -> 0 us
    all_to_all x2 -> x0, blocking collectives: 37.9 us -> none  [sum_at_owner(): lax.all_to_all(parts, axis, split_axis=0, concat_axis=0, tiled=True)]
    pallas_call x0 -> x1, Pallas kernels: none -> 29.6 us  [shards(): pl.pallas_call(body, out_shape=jax.ShapeDtypeStruct((OWN, EOFS), F32), in...]
    unnamed x23 -> x1, local copies, waits for them, and re-layouts: 30 us -> 1.32 us
    dot_general x9 -> x0, matrix products: 22.8 us -> none  [the longest x3 14.2 us: shards(): jnp.einsum('tpsx,tpsc->txc', weights[grid_id], blocks, preferred_element_...]
    sub x6 -> x0, local copies, waits for them, and re-layouts: 22.2 us -> none  [shards(): by_model - jnp.mean(by_model, axis=3, keepdims=True)]
    dot_general x3 -> x0, local copies, waits for them, and re-layouts: 19.8 us -> none  [shards(): jnp.einsum('tpsx,tpsc->txc', weights[grid_id], blocks, preferred_element_...]
    reduce_sum x8 -> x0, other arithmetic: 12.7 us -> none  [the longest x3 11.3 us: shards(): jnp.mean(by_model, axis=3, keepdims=True)]
    convert_element_type x3 -> x0, other arithmetic: 12.7 us -> none  [shards(): (by_model - jnp.mean(by_model, axis=3, keepdims=True)).astype(jnp.bfloat16)]
  transfers between devices with their start and end apart: 2 -> 0, of which waited for: 0 -> 0; matrix products, arithmetic and copies ran while one was open for 9% -> 0% of each run, Pallas kernels for 0% -> 0%
where the time goes in v2:
time: 31.1 us; the launch traced here: 30.9 us
  Pallas kernels  29.6 us (95%)
  local copies, waits for them, and re-layouts  1.32 us (4%)
    pallas_call x1, Pallas kernels, shards(): pl.pallas_call(body, out_shape=jax.ShapeDtypeStruct((OWN, EOFS), F32), in...  29.6 us
    unnamed x1, local copies, waits for them, and re-layouts  1.32 us

profile of v2, /device:TPU:1, one launch (start us, length us, event | category | flops | bytes accessed | tf_op | source)
XLA Modules:
  0.0 30.9 jit_solution(4849388416467788724)
XLA Ops:
  0.0 29.6 %shard_map.64 = f32[9,200]{1,0:T(8,128)} custom-call(s32[48,128]{1,0:T(8,128)} %bitcast.10, s32[3,8,32]{2,1,0:T(8,128)} %bitcast.11, s32[3,32]{1,0:T(4,128)} %counts.1, bf16[48,32,384]{2,1,0:T(8,128)(2,1)} %bitcast.8, bf16[3,32,256,128]{3,2,1,0:T(8,128)(2,1)} %bitcast.7, bf16[200,4096]{1,0:T(8,128)(2,1)} %eofs.1), custom_call_target="tpu_custom_call" | custom-call | tf_op jit(solution)/shard_map/pallas_call | solution.py:289
  29.6 1.3 %copy.8 = f32[200,9]{0,1:T(8,128)} copy(f32[200,9]{0,1:T(8,128)} %bitcast.9) | data formatting | bytes 14400

commit v3 on v2

v3 whole, which is shorter than its diff:
```python
import jax
import jax.numpy as jnp
from jax import lax
from jax.experimental import pallas as pl
from jax.experimental.pallas import tpu as pltpu
from jax.sharding import PartitionSpec as P

MESH = pl.DeviceIdType.MESH
GRIDS, TILES, PAIRS, TS, TT = 3, 32, 8, 32, 128
STILES, REQ, CAP, COLS, EOFS = 16, 16, 8, 384, 200
N_LAT, N_LON = 4, 32
DEVS = N_LAT * N_LON
OWN = 9
MONTHS = 24
GROUPS = 8
SPLIT = 4
F32 = jnp.float32
BF16 = jnp.bfloat16
PHASES = ((0, 0, 5), (1, 5, 10), (2, 10, 16))
CHIPS = DEVS // 2


def body(
    requests, slots, counts, fields, weights, eofs, out,
    wanted, slot_v, count_v, fld, send, halo_0, halo_1, halo_2, wv, ev, gv, lhs, av, pv, tails,
    pairbox, twinbox, outbox, inbox,
    sem_i, sem_f, sem_w, sem_e, halo_s, halo_r, x_sem, z_sem, pair_s, pair_r, rs_s, rs_r,
):
    lat = lax.axis_index("lat")
    lon = lax.axis_index("lon")
    me = lat * N_LON + lon
    core = lon & 1
    chip = me >> 1
    right = (lon + 1) & 31
    left = (lon + 31) & 31
    halos = (halo_0, halo_1, halo_2)

    barrier = pltpu.get_barrier_semaphore()

    def greet(sem, to_lat, to_lon):
        pl.semaphore_signal(sem, inc=1, device_id=(to_lat, to_lon), device_id_type=MESH)

    with jax.named_scope("greet"):
        greet(barrier, lat, left)
        greet(barrier, lat, right)
        for step in range(1, 8):
            greet(barrier, lat, lon ^ step)
        for step in range(1, 4):
            greet(barrier, lat, lon ^ (step * 8))
            greet(barrier, lat ^ step, lon)

        inputs = [
            pltpu.make_async_copy(requests, wanted, sem_i.at[0]),
            pltpu.make_async_copy(slots, slot_v, sem_i.at[1]),
            pltpu.make_async_copy(counts, count_v, sem_i.at[2]),
        ]
        for copy in inputs:
            copy.start()
        field_copy = pltpu.make_async_copy(fields, fld, sem_f)
        field_copy.start()

    def e_copy(c):
        return pltpu.make_async_copy(
            eofs.at[:, pl.ds(pl.multiple_of(c * 512, 512), 512)], ev.at[c, pl.ds(0, EOFS)], sem_e.at[c]
        )

    def w_copy(c):
        return [
            pltpu.make_async_copy(weights.at[:, c * 4 + tt], wv.at[c, tt], sem_w.at[c, tt])
            for tt in range(4)
        ]

    @pl.loop(0, GROUPS)
    def _(c):
        ev[c, 192:256, :] = jnp.zeros((64, 512), BF16)
        e_copy(c).start()
        for copy in w_copy(c):
            copy.start()

    with jax.named_scope("inputs"):
        for copy in inputs:
            copy.wait()

    def mine_of(g, device):
        packed = jnp.int32(0)
        place = jnp.int32(1)
        for j in range(REQ):
            source = wanted[g * REQ + j, device]
            mine = (source >> 4) == me
            packed = packed + jnp.where(mine, (source & 15) * place, 0)
            place = jnp.where(mine, place * 16, place)
        return [lax.shift_right_logical(packed, jnp.int32(4 * r)) & 15 for r in range(CAP)]

    with jax.named_scope("pick"):
        picked = [[mine_of(g, lat * N_LON + to) for g in range(GRIDS)] for to in (right, left)]

    with jax.named_scope("gather"):
        with jax.named_scope("wait_f"):
            field_copy.wait()
        for g in range(GRIDS):
            for way in range(2):
                for r in range(CAP):
                    send[way, g, r] = fld[g * STILES + picked[way][g][r]]

    def halo_copy(way, g):
        return pltpu.make_async_remote_copy(
            src_ref=send.at[way, g],
            dst_ref=halos[g].at[way],
            send_sem=halo_s.at[way, g],
            recv_sem=halo_r.at[way, g],
            device_id=(lat, right if way == 0 else left),
            device_id_type=MESH,
        )

    def project(c):
        rows = lax.broadcasted_iota(jnp.int32, (128, 256), 0).astype(F32)
        for g in range(GRIDS):
            hit = rows == codes[g : g + 1, c * 256 : (c + 1) * 256]
            lhs[g * GROUPS + c] = jnp.where(hit, 1.0, 0.0).astype(BF16)
        for tt in range(4):
            basis = ev[c, :, tt * TT : (tt + 1) * TT]
            made = lax.dot_general(
                wv[c, tt].reshape(GRIDS * 256, TT), basis, (((1,), (1,)), ((), ())),
                preferred_element_type=F32,
            )
            wide = made.reshape(GRIDS, 8, 4, 8, 256)
            for g in range(GRIDS):
                for q in range(4):
                    gv[g, c, q, pl.ds(tt * 8, 8)] = wide[g, :, q]

    def arrived(c):
        e_copy(c).wait()
        for copy in w_copy(c):
            copy.wait()

    with jax.named_scope("barrier"):
        pl.semaphore_wait(barrier, 15)
        for g, _, _ in PHASES:
            halo_copy(0, g).start()
            halo_copy(1, g).start()
        for step in range(1, 4):
            greet(x_sem, lat, lon ^ (step * 8))

    with jax.named_scope("wait_a"):
        for c in range(SPLIT):
            arrived(c)

    with jax.named_scope("project_a"):
        live = lax.broadcasted_iota(jnp.int32, (GRIDS, PAIRS, TILES), 1) < count_v[...][:, None, :]
        marked = jnp.where(live, slot_v[...] + 1, 0).astype(F32)
        marked = marked.reshape(GRIDS * PAIRS, TILES).astype(BF16)
        lane = lax.broadcasted_iota(jnp.int32, (TILES, TILES * 64), 1)
        tile = lax.broadcasted_iota(jnp.int32, (TILES, TILES * 64), 0)
        spread = jnp.where((lane >> 6) == tile, 1.0, 0.0).astype(BF16)
        codes = jnp.dot(marked, spread, preferred_element_type=F32)
        codes = codes.reshape(GRIDS, PAIRS, TILES * 64)
        lane = lax.broadcasted_iota(jnp.int32, (PAIRS, TILES * 64), 1)
        pair = lax.broadcasted_iota(jnp.int32, (PAIRS, TILES * 64), 0)
        codes = jnp.sum(jnp.where(((lane >> 3) & 7) == pair, codes, 0.0), axis=1)
        row = (lax.broadcasted_iota(jnp.int32, (GRIDS, TILES * 64), 1) & 7).astype(F32)
        codes = codes * 8.0 + (row - 8.0)
        for c in range(SPLIT):
            project(c)

    with jax.named_scope("barrier2"):
        pl.semaphore_wait(x_sem, 3)
        for step in range(1, 4):
            greet(z_sem, lat ^ step, lon)

    with jax.named_scope("wait_b"):
        for c in range(SPLIT, GROUPS):
            arrived(c)

    with jax.named_scope("project_b"):
        for c in range(SPLIT, GROUPS):
            project(c)

    lanes = lax.broadcasted_iota(jnp.int32, (8, 128), 1)

    def pair_copy(turn):
        _, start, stop = PHASES[turn]
        return pltpu.make_async_remote_copy(
            src_ref=pairbox.at[1 - core, pl.ds(start * 4, (stop - start) * 4)],
            dst_ref=twinbox.at[pl.ds(start * 4, (stop - start) * 4)],
            send_sem=pair_s.at[turn],
            recv_sem=pair_r.at[turn],
            device_id=(lat, lon ^ 1),
            device_id_type=MESH,
        )

    def owner_copy(place, to_core, slot):
        owner = place * 2 + to_core
        return pltpu.make_async_remote_copy(
            src_ref=outbox.at[place],
            dst_ref=inbox.at[slot],
            send_sem=rs_s,
            recv_sem=rs_r,
            device_id=(owner >> 5, owner & 31),
            device_id_type=MESH,
        )

    def deliver(turn):
        _, start, stop = PHASES[turn]
        count = stop - start
        with jax.named_scope(f"pair{turn}"):
            pair_copy(turn).wait_recv()
            if turn == 0:
                pl.semaphore_wait(z_sem, 3)
        with jax.named_scope(f"send{turn}"):
            for i in range(start * 4, stop * 4):
                outbox[i] = (pairbox[core, i] + twinbox[i]).astype(BF16)
            first_group = lax.rem(chip >> 2, count)
            for k in range(count):
                group = k + first_group
                group = start + group - jnp.where(group >= count, count, 0)
                own = group == chip >> 2
                place = group * 4 + (chip & 3)
                owner_copy(
                    place, jnp.where(own, 1 - core, core), jnp.where(own, CHIPS, chip)
                ).start()
                for j in range(1, 4):
                    owner_copy(group * 4 + ((chip & 3) ^ j), core, chip).start()

    def landed(g):
        with jax.named_scope(f"halo{g}"):
            halo_copy(0, g).wait_recv()
            halo_copy(1, g).wait_recv()

    for turn, (g, start, stop) in enumerate(PHASES):
        if turn > 0:
            landed(g)
        with jax.named_scope(f"addup{g}"):

            @pl.loop(0, 4, unroll=True)
            def _(q):
                total = jnp.zeros((128, 256), F32)
                for c in range(GROUPS):
                    terms = gv[g, c, q].reshape(256, 256)
                    high = terms.astype(BF16)
                    low = (terms - high.astype(F32)).astype(BF16)
                    chosen = lhs[g * GROUPS + c]
                    total += jnp.dot(chosen, high, preferred_element_type=F32)
                    total += jnp.dot(chosen, low, preferred_element_type=F32)
                av[g, :, q] = total.reshape(REQ, 8, 256)

        if turn == 0:
            landed(g)
        if turn > 0:
            deliver(turn - 1)
        with jax.named_scope(f"product{g}"):
            product = jnp.zeros((COLS, 256), F32)
            seen_left = jnp.int32(0)
            seen_right = jnp.int32(0)
            for half in range(2):
                blocks = []
                for j in range(half * 8, half * 8 + 8):
                    source = wanted[g * REQ + j, me]
                    owner = source >> 4
                    on_left = owner == lat * N_LON + left
                    on_me = owner == me
                    from_left = halos[g][0, seen_left & 7]
                    from_right = halos[g][1, seen_right & 7]
                    from_me = fld[g * STILES + (source & 15)]
                    blocks.append(
                        jnp.where(on_me, from_me, jnp.where(on_left, from_left, from_right))
                    )
                    seen_left = seen_left + jnp.where(on_left, 1, 0)
                    seen_right = seen_right + jnp.where(on_left | on_me, 0, 1)
                turned = jnp.concatenate(blocks, axis=0).T
                source = av[g, pl.ds(half * 8, 8)].reshape(256, 256)
                high = source.astype(BF16)
                low = (source - high.astype(F32)).astype(BF16)
                product += jnp.dot(turned, high, preferred_element_type=F32)
                product += jnp.dot(turned, low, preferred_element_type=F32)
            by_model = product.reshape(COLS // MONTHS, MONTHS, 256)
            centred = by_model - jnp.sum(by_model, axis=1, keepdims=True) * (1.0 / MONTHS)
            centred = centred.reshape(COLS, 256)
            pv[0, pl.ds(g * COLS, COLS), :] = centred[:, :128]
            pv[1, pl.ds(g * COLS, COLS), :] = centred[:, 128:]

        with jax.named_scope(f"pack{g}"):

            @pl.loop(start, stop, unroll=True)
            def _(i):
                base = pl.multiple_of(i * 72, 8)
                last = [pv[half, pl.ds(base + 8, 8, stride=9), :] for half in range(2)]
                for r, (half, shift) in enumerate(((0, 72), (0, 16), (0, 88), (1, 72), (1, 16))):
                    tails[i, pl.ds(r, 8, stride=8), :] = pltpu.roll(last[half], shift, 1)
                for r in range(5, 8):
                    tails[i, pl.ds(r, 8, stride=8), :] = jnp.zeros((8, 128), F32)
                for j in range(8):
                    first = pv[0, pl.ds(base + 9 * j, 8), :]
                    second = jnp.where(
                        lanes < 72, pv[1, pl.ds(base + 9 * j, 8), :], tails[i, 8 * j : 8 * j + 8, :]
                    )
                    pairbox[j & 1, i * 4 + j // 2] = jnp.concatenate([first, second], axis=0)

            pair_copy(turn).start()

    deliver(GRIDS - 1)

    with jax.named_scope("arrive"):
        inbox[chip] = outbox[chip]
        everything = pltpu.make_async_remote_copy(
            src_ref=outbox,
            dst_ref=inbox.at[pl.ds(0, CHIPS)],
            send_sem=rs_s,
            recv_sem=rs_r,
            device_id=(lat, right),
            device_id_type=MESH,
        )
        everything.wait_recv()
    with jax.named_scope("final"):
        total = jnp.zeros((16, 128), F32)
        for i in range(CHIPS):
            total += inbox[i].astype(F32)
        first, second = total[:8], total[8:]
        by_56, by_112, by_40 = (pltpu.roll(second, shift, 1) for shift in (56, 112, 40))
        lane = lanes[:1]
        last_0 = jnp.where(lane < 56, by_56[0:1], jnp.where(lane < 112, by_112[1:2], by_40[2:3]))
        last_1 = jnp.where(lane < 56, by_56[3:4], by_112[4:5])
        out[0:8, 0:128] = first
        out[0:8, 128:EOFS] = second[:, : EOFS - 128]
        out[8:9, 0:128] = last_0
        out[8:9, 128:EOFS] = last_1[:, : EOFS - 128]

    with jax.named_scope("drain"):
        everything.wait_send()
        for g in range(GRIDS):
            halo_copy(0, g).wait_send()
            halo_copy(1, g).wait_send()
            pair_copy(g).wait_send()


def shards(fields, weights, pair_slots, pair_counts, requests, eofs):
    return pl.pallas_call(
        body,
        out_shape=pltpu.VMEM((OWN, EOFS), F32),
        in_specs=[pl.BlockSpec(memory_space=pl.ANY)] * 6,
        out_specs=pl.BlockSpec(memory_space=pltpu.VMEM),
        scratch_shapes=[
            pltpu.SMEM((GRIDS * REQ, DEVS), jnp.int32),
            pltpu.VMEM((GRIDS, PAIRS, TILES), jnp.int32),
            pltpu.VMEM((GRIDS, TILES), jnp.int32),
            pltpu.VMEM((GRIDS * STILES, TS, COLS), BF16),
            pltpu.VMEM((2, GRIDS, CAP, TS, COLS), BF16),
            pltpu.VMEM((2, CAP, TS, COLS), BF16),
            pltpu.VMEM((2, CAP, TS, COLS), BF16),
            pltpu.VMEM((2, CAP, TS, COLS), BF16),
            pltpu.VMEM((GROUPS, 4, GRIDS, 256, TT), BF16),
            pltpu.VMEM((GROUPS, 256, 512), BF16),
            pltpu.VMEM((GRIDS, GROUPS, 4, 32, 8, 256), F32),
            pltpu.VMEM((GRIDS * GROUPS, 128, 256), BF16),
            pltpu.VMEM((GRIDS, REQ, 4, 8, 256), F32),
            pltpu.VMEM((2, GRIDS * COLS + 8, 128), F32),
            pltpu.VMEM((16, 64, 128), F32),
            pltpu.VMEM((2, CHIPS, 16, 128), F32),
            pltpu.VMEM((CHIPS, 16, 128), F32),
            pltpu.VMEM((CHIPS, 16, 128), BF16),
            pltpu.VMEM((CHIPS + 1, 16, 128), BF16),
            pltpu.SemaphoreType.DMA((3,)),
            pltpu.SemaphoreType.DMA,
            pltpu.SemaphoreType.DMA((GROUPS, 4)),
            pltpu.SemaphoreType.DMA((GROUPS,)),
            pltpu.SemaphoreType.DMA((2, GRIDS)),
            pltpu.SemaphoreType.DMA((2, GRIDS)),
            pltpu.SemaphoreType.REGULAR,
            pltpu.SemaphoreType.REGULAR,
            pltpu.SemaphoreType.DMA((GRIDS,)),
            pltpu.SemaphoreType.DMA((GRIDS,)),
            pltpu.SemaphoreType.DMA,
            pltpu.SemaphoreType.DMA,
        ],
        compiler_params=pltpu.CompilerParams(
            collective_id=0, has_side_effects=True, vmem_limit_bytes=56 * 1024 * 1024
        ),
    )(
        requests.transpose(0, 2, 1).reshape(GRIDS * REQ, DEVS),
        pair_slots.transpose(0, 2, 1),
        pair_counts,
        fields.reshape(GRIDS * STILES, TS, COLS),
        weights.reshape(GRIDS, TILES, PAIRS * TS, TT),
        eofs,
    ).T


def solution(mesh):
    return jax.shard_map(
        shards,
        mesh=mesh,
        in_specs=(
            P(None, ("lat", "lon"), None, None),
            P(None, ("lat", "lon"), None, None, None),
            P(None, ("lat", "lon"), None),
            P(None, ("lat", "lon")),
            P(),
            P(None, ("lat", "lon")),
        ),
        out_specs=P(None, ("lat", "lon")),
        check_vma=False,
    )
```

time: 31.1 us -> 24.8 us (0.80)
  the two profiles are of different devices: /device:TPU:1 before, /device:TPU:96 now
where the time goes in v3:
time: 24.8 us; the launch traced here: 24.7 us
  Pallas kernels  24.1 us (97%)
  local copies, waits for them, and re-layouts  0.61 us (2%)
    pallas_call x1, Pallas kernels, shards(): pl.pallas_call(body, out_shape=pltpu.VMEM((OWN, EOFS), F32), in_specs=[pl...  24.1 us
    unnamed x1, local copies, waits for them, and re-layouts  0.61 us

profile of v3, /device:TPU:96, one launch (start us, length us, event | category | flops | bytes accessed | tf_op | source)
XLA Modules:
  0.0 24.7 jit_solution(9154798393001227426)
XLA Ops:
  0.0 24.1 %shard_map.64 = f32[9,200]{1,0:T(8,128)S(1)} custom-call(s32[48,128]{1,0:T(8,128)} %bitcast.10, s32[3,8,32]{2,1,0:T(8,128)} %bitcast.11, s32[3,32]{1,0:T(4,128)} %counts.1, bf16[48,32,384]{2,1,0:T(8,128)(2,1)} %bitcast.9, bf16[3,32,256,128]{3,2,1,0:T(8,128)(2,1)} %bitcast.8, bf16[200,4096]{1,0:T(8,128)(2,1)} %eofs.1), custom_call_target="tpu_custom_call" | custom-call | tf_op jit(solution)/shard_map/pallas_call | solution.py:336
  24.1 0.6 %copy.8 = f32[200,9]{0,1:T(8,128)} copy(f32[200,9]{0,1:T(8,128)S(1)} %bitcast.7) | data formatting | bytes 14400

commit v4 on v3

--- a/solution.py
+++ b/solution.py
@@ -13,6 +13,7 @@
 OWN = 9
 MONTHS = 24
 GROUPS = 8
+HUB = 1
 SPLIT = 4
 F32 = jnp.float32
 BF16 = jnp.bfloat16
@@ -24,16 +25,21 @@
     requests, slots, counts, fields, weights, eofs, out,
     wanted, slot_v, count_v, fld, send, halo_0, halo_1, halo_2, wv, ev, gv, lhs, av, pv, tails,
     pairbox, twinbox, outbox, inbox,
-    sem_i, sem_f, sem_w, sem_e, halo_s, halo_r, x_sem, z_sem, pair_s, pair_r, rs_s, rs_r,
+    sem_i, sem_f, sem_w, sem_e, halo_s, halo_r, x_sem, z_sem, g_sem, own_sem, pair_s, pair_r, rs_s, rs_r,
 ):
     lat = lax.axis_index("lat")
     lon = lax.axis_index("lon")
     me = lat * N_LON + lon
     core = lon & 1
+    hub = (lon & 7) == HUB
     chip = me >> 1
     right = (lon + 1) & 31
     left = (lon + 31) & 31
     halos = (halo_0, halo_1, halo_2)
+
+    def fence():
+        pl.semaphore_signal(own_sem, inc=1)
+        pl.semaphore_wait(own_sem, 1)
 
     barrier = pltpu.get_barrier_semaphore()
 
@@ -45,9 +51,12 @@
         greet(barrier, lat, right)
         for step in range(1, 8):
             greet(barrier, lat, lon ^ step)
-        for step in range(1, 4):
-            greet(barrier, lat, lon ^ (step * 8))
-            greet(barrier, lat ^ step, lon)
+
+        @pl.when(hub)
+        def _():
+            for step in range(1, 4):
+                greet(barrier, lat, lon ^ (step * 8))
+                greet(barrier, lat ^ step, lon)
 
         inputs = [
             pltpu.make_async_copy(requests, wanted, sem_i.at[0]),
@@ -126,7 +135,10 @@
             wide = made.reshape(GRIDS, 8, 4, 8, 256)
             for g in range(GRIDS):
                 for q in range(4):
-                    gv[g, c, q, pl.ds(tt * 8, 8)] = wide[g, :, q]
+                    terms = wide[g, :, q].reshape(64, 256)
+                    high = terms.astype(BF16)
+                    gv[g, c, q, 0, pl.ds(tt * 64, 64), :] = high
+                    gv[g, c, q, 1, pl.ds(tt * 64, 64), :] = (terms - high.astype(F32)).astype(BF16)
 
     def arrived(c):
         e_copy(c).wait()
@@ -134,18 +146,21 @@
             copy.wait()
 
     with jax.named_scope("barrier"):
-        pl.semaphore_wait(barrier, 15)
+        pl.semaphore_wait(barrier, jnp.where(hub, 15, 9))
         for g, _, _ in PHASES:
             halo_copy(0, g).start()
             halo_copy(1, g).start()
-        for step in range(1, 4):
-            greet(x_sem, lat, lon ^ (step * 8))
-
-    with jax.named_scope("wait_a"):
-        for c in range(SPLIT):
+
+        @pl.when(hub)
+        def _():
+            for step in range(1, 4):
+                greet(x_sem, lat, lon ^ (step * 8))
+
+    with jax.named_scope("wait_0"):
+        for c in range(0, 2):
             arrived(c)
 
-    with jax.named_scope("project_a"):
+    with jax.named_scope("project_0"):
         live = lax.broadcasted_iota(jnp.int32, (GRIDS, PAIRS, TILES), 1) < count_v[...][:, None, :]
         marked = jnp.where(live, slot_v[...] + 1, 0).astype(F32)
         marked = marked.reshape(GRIDS * PAIRS, TILES).astype(BF16)
@@ -159,20 +174,39 @@
         codes = jnp.sum(jnp.where(((lane >> 3) & 7) == pair, codes, 0.0), axis=1)
         row = (lax.broadcasted_iota(jnp.int32, (GRIDS, TILES * 64), 1) & 7).astype(F32)
         codes = codes * 8.0 + (row - 8.0)
-        for c in range(SPLIT):
+        for c in range(0, 2):
             project(c)
 
     with jax.named_scope("barrier2"):
-        pl.semaphore_wait(x_sem, 3)
-        for step in range(1, 4):
-            greet(z_sem, lat ^ step, lon)
-
-    with jax.named_scope("wait_b"):
-        for c in range(SPLIT, GROUPS):
+
+        @pl.when(hub)
+        def _():
+            pl.semaphore_wait(x_sem, 3)
+            for step in range(1, 4):
+                greet(z_sem, lat ^ step, lon)
+
+    with jax.named_scope("wait_1"):
+        for c in range(2, 5):
             arrived(c)
 
-    with jax.named_scope("project_b"):
-        for c in range(SPLIT, GROUPS):
+    with jax.named_scope("project_1"):
+        for c in range(2, 5):
+            project(c)
+
+    with jax.named_scope("barrier3"):
+
+        @pl.when(hub)
+        def _():
+            pl.semaphore_wait(z_sem, 3)
+            for step in range(1, 8):
+                greet(g_sem, lat, lon ^ step)
+
+    with jax.named_scope("wait_2"):
+        for c in range(5, 8):
+            arrived(c)
+
+    with jax.named_scope("project_2"):
+        for c in range(5, 8):
             project(c)
 
     lanes = lax.broadcasted_iota(jnp.int32, (8, 128), 1)
@@ -205,7 +239,11 @@
         with jax.named_scope(f"pair{turn}"):
             pair_copy(turn).wait_recv()
             if turn == 0:
-                pl.semaphore_wait(z_sem, 3)
+
+                @pl.when(jnp.logical_not(hub))
+                def _():
+                    pl.semaphore_wait(g_sem, 1)
+
         with jax.named_scope(f"send{turn}"):
             for i in range(start * 4, stop * 4):
                 outbox[i] = (pairbox[core, i] + twinbox[i]).astype(BF16)
@@ -227,27 +265,23 @@
             halo_copy(1, g).wait_recv()
 
     for turn, (g, start, stop) in enumerate(PHASES):
-        if turn > 0:
-            landed(g)
         with jax.named_scope(f"addup{g}"):
+            fence()
 
             @pl.loop(0, 4, unroll=True)
             def _(q):
                 total = jnp.zeros((128, 256), F32)
                 for c in range(GROUPS):
-                    terms = gv[g, c, q].reshape(256, 256)
-                    high = terms.astype(BF16)
-                    low = (terms - high.astype(F32)).astype(BF16)
                     chosen = lhs[g * GROUPS + c]
-                    total += jnp.dot(chosen, high, preferred_element_type=F32)
-                    total += jnp.dot(chosen, low, preferred_element_type=F32)
+                    total += jnp.dot(chosen, gv[g, c, q, 0], preferred_element_type=F32)
+                    total += jnp.dot(chosen, gv[g, c, q, 1], preferred_element_type=F32)
                 av[g, :, q] = total.reshape(REQ, 8, 256)
 
-        if turn == 0:
-            landed(g)
+        landed(g)
         if turn > 0:
             deliver(turn - 1)
         with jax.named_scope(f"product{g}"):
+            fence()
             product = jnp.zeros((COLS, 256), F32)
             seen_left = jnp.int32(0)
             seen_right = jnp.int32(0)
@@ -349,7 +383,7 @@
             pltpu.VMEM((2, CAP, TS, COLS), BF16),
             pltpu.VMEM((GROUPS, 4, GRIDS, 256, TT), BF16),
             pltpu.VMEM((GROUPS, 256, 512), BF16),
-            pltpu.VMEM((GRIDS, GROUPS, 4, 32, 8, 256), F32),
+            pltpu.VMEM((GRIDS, GROUPS, 4, 2, 256, 256), BF16),
             pltpu.VMEM((GRIDS * GROUPS, 128, 256), BF16),
             pltpu.VMEM((GRIDS, REQ, 4, 8, 256), F32),
             pltpu.VMEM((2, GRIDS * COLS + 8, 128), F32),
@@ -364,6 +398,8 @@
             pltpu.SemaphoreType.DMA((GROUPS,)),
             pltpu.SemaphoreType.DMA((2, GRIDS)),
             pltpu.SemaphoreType.DMA((2, GRIDS)),
+            pltpu.SemaphoreType.REGULAR,
+            pltpu.SemaphoreType.REGULAR,
             pltpu.SemaphoreType.REGULAR,
             pltpu.SemaphoreType.REGULAR,
             pltpu.SemaphoreType.DMA((GRIDS,)),

time: 24.8 us -> 23.1 us (0.931)
  the two profiles are of different devices: /device:TPU:96 before, /device:TPU:1 now
where the time goes in v4:
time: 23.1 us; the launch traced here: 23 us
  Pallas kernels  22.3 us (97%)
  local copies, waits for them, and re-layouts  0.61 us (3%)
    pallas_call x1, Pallas kernels, shards(): pl.pallas_call(body, out_shape=pltpu.VMEM((OWN, EOFS), F32), in_specs=[pl...  22.3 us
    unnamed x1, local copies, waits for them, and re-layouts  0.61 us

profile of v4, /device:TPU:1, one launch (start us, length us, event | category | flops | bytes accessed | tf_op | source)
XLA Modules:
  0.0 23.0 jit_solution(3126607865269976331)
XLA Ops:
  0.0 22.3 %shard_map.64 = f32[9,200]{1,0:T(8,128)S(1)} custom-call(s32[48,128]{1,0:T(8,128)} %bitcast.10, s32[3,8,32]{2,1,0:T(8,128)} %bitcast.11, s32[3,32]{1,0:T(4,128)} %counts.1, bf16[48,32,384]{2,1,0:T(8,128)(2,1)} %bitcast.9, bf16[3,32,256,128]{3,2,1,0:T(8,128)(2,1)} %bitcast.8, bf16[200,4096]{1,0:T(8,128)(2,1)} %eofs.1), custom_call_target="tpu_custom_call" | custom-call | tf_op jit(solution)/shard_map/pallas_call | solution.py:370
  22.4 0.6 %copy.8 = f32[200,9]{0,1:T(8,128)} copy(f32[200,9]{0,1:T(8,128)S(1)} %bitcast.7) | data formatting | bytes 14400
